TPU v7x, 256 devices: a whole 4x4x8 slice. The times are simulated.
256 devices in a mesh: gy: 64 (over z, y_lo, x), gx: 4 (over y_hi, core).
Axes of the slice: x: 4, y: 4 (y_hi: 2, y_lo: 2; y = y_hi * 2 + y_lo), z: 8, core: 2. Of those that a mesh axis runs over, the one named last changes fastest.
Arguments:
- fields: float32 [8, 64, 2048, 128], P(None, 'gx', 'gy'), may hold values from -6 to 6
- shifts: int32 [64], P('gx'), may hold values from 0 to 2047
- fraction: float32 [64], P('gx'), may hold values from 0.4 to 0.6
Outputs:
- remapped: float32 [8, 64, 2048, 128], P(None, 'gx', 'gy')
- stress: float32 [2, 128], replicated
All inputs are finite; a program needn't handle non-finite values.
Results may differ from a plain program's by a relative error of at most 0.0003.
Values sent between devices are 32-bit elements; how exact they have to be, the bound alone decides.
No kernel may reach another device: no remote copies, remote signals or barrier semaphores. Data moves between devices by JAX's collectives and lax.ppermute only.
A program may use at most 64 MiB of HBM per device.

v0:
```python
from functools import partial
import math

import jax
import jax.numpy as jnp
from jax import lax
from jax.sharding import Mesh
from jax.sharding import PartitionSpec as P

GY = ("gy_0", "gy_1", "gy_2")
GY_GX = ("gy_0", "gy_1", "gy_2", "gx_0", "gx_1")
GX = ("gx_0", "gx_1")


def over_axes(shard, axes):
    for axis in axes:
        shard = lax.psum(shard, axis)
    return shard


def remap_cells(extended, fraction, length, stride):

    def cells(first, number):
        return extended[..., first * stride : (first + number) * stride]

    interface = (
        7.0 * (cells(1, length + 2) + cells(2, length + 2))
        - (cells(0, length + 2) + cells(3, length + 2))
    ) / 12.0
    left_edge = interface[..., : (length + 1) * stride]
    right_edge = interface[..., stride:]
    centre = cells(2, length + 1)
    slope = right_edge - left_edge
    curve = 6.0 * centre - 3.0 * (left_edge + right_edge)
    outflow = fraction * (
        right_edge - 0.5 * fraction * (slope - (1.0 - 2.0 * fraction / 3.0) * curve)
    )
    return cells(3, length) - outflow[..., stride:] + outflow[..., : length * stride]


def cut_flat(column, offset, length):
    return lax.dynamic_slice_in_dim(column, offset, length, 0)


def on_device(fields, shifts, fraction):
    components = fields.shape[0]
    columns = fields.shape[1]
    slab_cells = fields.shape[2]
    vertical = fields.shape[3]
    loop_size = lax.axis_size(GY)
    pair_count = components * columns
    stacked = fields.reshape(pair_count, slab_cells, vertical)
    gathered = lax.all_to_all(stacked, GY, split_axis=0, concat_axis=1, tiled=True)
    held = gathered.shape[0]
    azimuth = gathered.shape[1]
    pair_ids = lax.axis_index(GY) * held + jnp.arange(held, dtype=jnp.int32)
    column_ids = jnp.mod(pair_ids, columns)
    picker = column_ids[:, None] == jnp.arange(columns, dtype=jnp.int32)[None, :]
    pair_shift = jnp.sum(jnp.where(picker, shifts[None, :], 0), axis=1)
    pair_share = jnp.sum(jnp.where(picker, fraction[None, :], 0.0), axis=1)
    flat = gathered.reshape(held, azimuth * vertical)
    doubled = jnp.concatenate([flat, flat, flat[:, : 4 * vertical]], axis=1)
    starts = jnp.mod(-3 - pair_shift, azimuth) * vertical
    cutter = partial(cut_flat, length=(azimuth + 5) * vertical)
    extended = jax.vmap(cutter, in_axes=(0, 0), out_axes=0)(doubled, starts)
    moved = remap_cells(extended, pair_share[:, None], azimuth, vertical).reshape(
        held, azimuth, vertical
    )
    returned = lax.all_to_all(moved, GY, split_axis=1, concat_axis=0, tiled=True)
    remapped = returned.reshape(fields.shape)
    reynolds = jnp.sum(remapped[1] * remapped[2], axis=(0, 1))
    maxwell = -jnp.sum(remapped[5] * remapped[6], axis=(0, 1))
    partial_sums = jnp.stack([reynolds, maxwell])
    summed = over_axes(partial_sums, GY_GX)
    total_cells = columns * lax.axis_size(GX) * slab_cells * loop_size
    stress = summed / math.sqrt(total_cells)
    return (remapped, stress)


def solution(mesh):
    split = Mesh(mesh.devices.reshape(8, 2, 4, 2, 2), ("gy_0", "gy_1", "gy_2", "gx_0", "gx_1"))
    placed = (P(None, GX, GY, None), P(GX), P(GX))
    return jax.shard_map(
        on_device,
        mesh=split,
        in_specs=placed,
        out_specs=(P(None, GX, GY, None), P()),
        check_vma=False,
    )
```

profile of v0, /device:TPU:1, one launch (start us, length us, event | category | flops | bytes accessed | tf_op | source)
XLA Modules:
  0.0 243.2 jit_solution(561229231911816674)
XLA Ops:
  0.6 0.0 copy-start
  0.6 0.0 copy-start.1
  0.6 13.9 %all-to-all-start = ((f32[128,32,128]{2,1,0:T(8,128)}), f32[128,32,128]{2,1,0:T(8,128)}, u32[]{:S(2)}, u32[]{:S(2)}) async-start(f32[128,32,128]{2,1,0:T(8,128)} %bitcast.31), calls=%async_computation | async-start | bytes 4194304 | tf_op jit(solution)/shard_map/all_to_all | solution.py:53
  14.6 0.0 copy-done
  14.6 0.2 select_reduce_fusion.1
  14.8 0.1 copy.15
  14.9 0.0 copy-done.1
  14.9 0.2 select_reduce_fusion
  15.1 47.9 %all-to-all-done = f32[128,32,128]{2,1,0:T(8,128)} async-done(((f32[128,32,128]{2,1,0:T(8,128)}), f32[128,32,128]{2,1,0:T(8,128)}, u32[]{:S(2)}, u32[]{:S(2)}) %all-to-all-start) | async-done | bytes 2097184 | tf_op jit(solution)/shard_map/all_to_all | solution.py:53
  63.0 1.8 copy.14
  64.8 7.6 %copy.20 = f32[1,2,2048,128]{3,1,2,0:T(2,128)S(1)} copy(f32[1,2,2048,128]{3,2,1,0:T(8,128)S(1)} %bitcast.30) | data formatting | bytes 4194304
  72.4 20.4 %pad_maximum_fusion = f32[2,524800]{1,0:T(2,128)} fusion(f32[2,512]{1,0:T(2,128)S(1)} %slice.74, f32[2,262144]{1,0:T(2,128)S(1)} %bitcast.29), kind=kLoop, calls=%fused_computation.1 | loop fusion | flops 2099200 | bytes 6299648 | tf_op jit(solution)/shard_map/concatenate | solution.py:62
  92.9 42.1 %while.1 = (s32[]{:T(128)}, f32[2,524800]{1,0:T(2,128)}, s32[2,2]{1,0:T(2,128)S(1)}, f32[2,262784]{1,0:T(2,128)S(1)}, s32[]{:T(128)}, /*index=5*/s32[]{:T(128)}) while((s32[]{:T(128)}, f32[2,524800]{1,0:T(2,128)}, s32[2,2]{1,0:T(2,128)S(1)}, f32[2,262784]{1,0:T(2,128)S(1)}, s32[]{:T(128)}, /*index=5*/s32[]{:T(128)}) %tuple.30), condition=%wide.while_cond, body=%wide.while_body.sunk | while | flops 2 | bytes 4204657 | solution.py:42
  92.9 0.6 fusion.8
  93.4 5.1 %dynamic-slice.7 = f32[1,262784]{1,0:T(1,128)S(1)} dynamic-slice(f32[2,524800]{1,0:T(2,128)} %get-tuple-element.86, s32[]{:T(128)} %bitcast.24, s32[]{:T(128)} %bitcast.25), dynamic_slice_sizes={1,262784} | dynamic-slice | bytes 2102276 | tf_op jit(solution)/shard_map/vmap()/gather
  98.5 15.3 %dynamic-update-slice.3 = f32[2,262784]{1,0:T(2,128)S(1)} dynamic-update-slice(f32[2,262784]{1,0:T(2,128)S(1)} %get-tuple-element.82, f32[1,262784]{1,0:T(1,128)S(1)} %dynamic-slice.7, s32[]{:T(128)} %get-tuple-element.79, s32[]{:T(128)} %constant.64.clone.1..sunk) | dynamic-update-slice | bytes 2102276 | tf_op jit(solution)/shard_map/vmap()/gather
  113.8 0.6 fusion.8
  114.4 5.1 %dynamic-slice.7 = f32[1,262784]{1,0:T(1,128)S(1)} dynamic-slice(f32[2,524800]{1,0:T(2,128)} %get-tuple-element.86, s32[]{:T(128)} %bitcast.24, s32[]{:T(128)} %bitcast.25), dynamic_slice_sizes={1,262784} | dynamic-slice | bytes 2102276 | tf_op jit(solution)/shard_map/vmap()/gather
  119.5 15.4 %dynamic-update-slice.3 = f32[2,262784]{1,0:T(2,128)S(1)} dynamic-update-slice(f32[2,262784]{1,0:T(2,128)S(1)} %get-tuple-element.82, f32[1,262784]{1,0:T(1,128)S(1)} %dynamic-slice.7, s32[]{:T(128)} %get-tuple-element.79, s32[]{:T(128)} %constant.64.clone.1..sunk) | dynamic-update-slice | bytes 2102276 | tf_op jit(solution)/shard_map/vmap()/gather
  134.9 3.3 %subtract_multiply_fusion = f32[2,262400]{1,0:T(2,128)S(1)} fusion(f32[2,262784]{1,0:T(2,128)S(1)} %get-tuple-element.9), kind=kLoop, calls=%fused_computation.2 | loop fusion | flops 2624000 | bytes 10496000 | tf_op jit(solution)/shard_map/div | solution.py:26
  138.2 3.2 %subtract_multiply_fusion.1 = f32[2,262272]{1,0:T(2,128)S(1)} fusion(f32[2,262784]{1,0:T(2,128)S(1)} %get-tuple-element.9, f32[2,262400]{1,0:T(2,128)S(1)} %subtract_multiply_fusion, f32[2]{0:T(128)S(1)} %get-tuple-element.43, f32[2]{0:T(128)S(1)} %get-tuple-element.42, f32[2]{0:T(128)S(1)} %select_reduce_fusion), kind=kLoop, calls=%fused_computation.3 | loop fusion | flops 5245440 | bytes 8392728 | tf_op jit(solution)/shard_map/mul | solution.py:35
  141.5 2.0 fusion
  143.5 54.5 %all_to_all.30 = f32[2,2048,128]{2,0,1:T(2,128)S(1)} all-to-all(f32[2,2048,128]{2,0,1:T(2,128)S(1)} %fusion), channel_id=1, replica_groups=mesh['gy_0'=8,'gy_1'=2,'gy_2'=4,'gx_0'=2,'gx_1'=2] {'gy_0','gy_1','gy_2'}, dimensions={1} | all-to-all | bytes 4194304 | tf_op jit(solution)/shard_map/all_to_all | solution.py:69
  198.0 0.1 copy.16
  198.1 0.1 fusion.2
  198.2 1.5 copy.17
  199.8 12.7 %psum.35 = f32[2,128]{1,0:T(2,128)S(1)} all-reduce(f32[2,128]{1,0:T(2,128)S(1)} %pad_maximum_fusion.1), channel_id=1, replica_groups=mesh['gy_0'=8,'gy_1'=2,'gy_2'=4,'gx_0'=2,'gx_1'=2] {'gy_0'}, use_global_device_ids=true, to_apply=%region_4.5 | all-reduce | flops 256 | bytes 2048 | tf_op jit(solution)/shard_map/psum | solution.py:17
  212.4 3.8 %psum.36 = f32[2,128]{1,0:T(2,128)S(1)} all-reduce(f32[2,128]{1,0:T(2,128)S(1)} %psum.35), channel_id=1, replica_groups=mesh['gy_0'=8,'gy_1'=2,'gy_2'=4,'gx_0'=2,'gx_1'=2] {'gy_1'}, use_global_device_ids=true, to_apply=%region_5.6 | all-reduce | flops 256 | bytes 2048 | tf_op jit(solution)/shard_map/psum | solution.py:17
  216.2 8.2 %psum.37 = f32[2,128]{1,0:T(2,128)S(1)} all-reduce(f32[2,128]{1,0:T(2,128)S(1)} %psum.36), channel_id=1, replica_groups=mesh['gy_0'=8,'gy_1'=2,'gy_2'=4,'gx_0'=2,'gx_1'=2] {'gy_2'}, use_global_device_ids=true, to_apply=%region_6.7 | all-reduce | flops 256 | bytes 2048 | tf_op jit(solution)/shard_map/psum | solution.py:17
  224.4 5.3 %psum.38 = f32[2,128]{1,0:T(2,128)S(1)} all-reduce(f32[2,128]{1,0:T(2,128)S(1)} %psum.37), channel_id=1, replica_groups=mesh['gy_0'=8,'gy_1'=2,'gy_2'=4,'gx_0'=2,'gx_1'=2] {'gx_0'}, use_global_device_ids=true, to_apply=%region_7.8 | all-reduce | flops 256 | bytes 2048 | tf_op jit(solution)/shard_map/psum | solution.py:17
  229.7 12.9 %psum.39 = f32[2,128]{1,0:T(2,128)S(1)} all-reduce(f32[2,128]{1,0:T(2,128)S(1)} %psum.38), channel_id=1, replica_groups=mesh['gy_0'=8,'gy_1'=2,'gy_2'=4,'gx_0'=2,'gx_1'=2] {'gx_1'}, use_global_device_ids=true, to_apply=%region_8.9 | all-reduce | flops 256 | bytes 2048 | tf_op jit(solution)/shard_map/psum | solution.py:17
  242.6 0.6 broadcast_multiply_fusion
  (11 shorter events, 0.1 us)
Async XLA Ops:
  0.6 14.0 %copy-start = (s32[16]{0:T(128)S(1)}, s32[16]{0:T(128)}, u32[]{:S(2)}) copy-start(s32[16]{0:T(128)} %param.4) | copy-start | bytes 196
  0.6 14.3 %copy-start.1 = (f32[16]{0:T(128)S(1)}, f32[16]{0:T(128)}, u32[]{:S(2)}) copy-start(f32[16]{0:T(128)} %param.5) | copy-start | bytes 196
  0.6 62.4 %all-to-all-start = ((f32[128,32,128]{2,1,0:T(8,128)}), f32[128,32,128]{2,1,0:T(8,128)}, u32[]{:S(2)}, u32[]{:S(2)}) async-start(f32[128,32,128]{2,1,0:T(8,128)} %bitcast.31), calls=%async_computation | async-start | bytes 4194304 | tf_op jit(solution)/shard_map/all_to_all | solution.py:53
where the time goes:
time: 244 us; the launch traced here: 243 us
  blocking collectives  97.3 us (40%)
  local copies, waits for them, and re-layouts  53.1 us (22%)
  waiting for transfers between devices  47.9 us (20%)
  other arithmetic  30.1 us (12%)
  starting transfers between devices  13.9 us (6%)
    all_to_all x1, blocking collectives, on_device(): lax.all_to_all(moved, GY, split_axis=1, concat_axis=0, tiled=True)  54.5 us
    all_to_all x1, waiting for transfers between devices, on_device(): lax.all_to_all(stacked, GY, split_axis=0, concat_axis=1, tiled=True)  47.9 us
    psum x5, blocking collectives, over_axes(): shard = lax.psum(shard, axis)  42.8 us
    gather x8, local copies, waits for them, and re-layouts  42 us
    concatenate x1, other arithmetic, on_device(): doubled = jnp.concatenate([flat, flat, flat[:, :4 * vertical]], axis=1)  20.4 us
    all_to_all x1, starting transfers between devices, on_device(): lax.all_to_all(stacked, GY, split_axis=0, concat_axis=1, tiled=True)  13.9 us
    unnamed x7, local copies, waits for them, and re-layouts  7.7 us
  transfers between devices with their start and end apart: 1, of which 1 were waited for; matrix products, arithmetic and copies ran while one was open for 0% of the time, Pallas kernels for 0%

commit v1 on v0

v1 whole, which is shorter than its diff:
```python
from functools import partial
import math

import jax
import jax.numpy as jnp
from jax import lax
from jax.experimental import pallas as pl
from jax.experimental.pallas import tpu as pltpu
from jax.sharding import Mesh
from jax.sharding import PartitionSpec as P

GY = ("gy_0", "gy_1", "gy_2")
GX = ("gx_0", "gx_1")
PAD = 48
SCOPE = 16 << 20


def taps(c):
    h = 0.5 * c
    m = 1.0 - (2.0 / 3.0) * c
    right = c * (1.0 - h - 3.0 * h * m)
    left = c * (h - 3.0 * h * m)
    here = 6.0 * c * h * m
    a, b = 1.0 / 12.0, 7.0 / 12.0
    both = right - left
    return (
        -a * left,
        b * left - a * both,
        here + a * right + b * both + b * left,
        (1.0 - here) - b * right + b * both - a * left,
        -b * right - a * both,
        a * right,
    )


def field_of(team, member):
    return jnp.where(team < 2, 4 * team + 1 + member, 4 * (team - 2) + 3 * member)


def copy_block(source, target):
    target[...] = source[...].reshape(target.shape)


def pack(fields):
    _, columns, slab, vertical = fields.shape
    return pl.pallas_call(
        copy_block,
        grid=(4, 2),
        in_specs=[pl.BlockSpec((1, columns, slab, vertical), lambda t, m: (field_of(t, m), 0, 0, 0))],
        out_specs=pl.BlockSpec((1, columns, 1, slab, vertical), lambda t, m: (t, 0, m, 0, 0)),
        out_shape=jax.ShapeDtypeStruct((4, columns, 2, slab, vertical), fields.dtype),
        compiler_params=pltpu.CompilerParams(vmem_limit_bytes=SCOPE),
        name="pack",
    )(fields)


def unpack(packed):
    _, columns, _, slab, vertical = packed.shape
    return pl.pallas_call(
        copy_block,
        grid=(4, 2),
        in_specs=[pl.BlockSpec((1, columns, 1, slab, vertical), lambda t, m: (t, 0, m, 0, 0))],
        out_specs=pl.BlockSpec((1, columns, slab, vertical), lambda t, m: (field_of(t, m), 0, 0, 0)),
        out_shape=jax.ShapeDtypeStruct((8, columns, slab, vertical), packed.dtype),
        compiler_params=pltpu.CompilerParams(vmem_limit_bytes=SCOPE),
        name="unpack",
    )(packed)


def remap_kernel(place_ref, shifts_ref, fraction_ref, held_ref, moved_ref, sums_ref, column_ref):
    slabs, members, slab, vertical = held_ref.shape
    azimuth = slabs * slab
    place = place_ref[0]
    column = lax.rem(place, shifts_ref.shape[0])
    team = lax.div(place, shifts_ref.shape[0])
    shift = shifts_ref[column]
    weights = taps(fraction_ref[column])

    def fill(g, carry):
        for m in range(members):
            column_ref[m, pl.ds(pl.multiple_of(g * slab, slab), slab), :] = held_ref[g, m]
        return carry

    lax.fori_loop(0, slabs, fill, 0, unroll=4)
    for m in range(members):
        column_ref[m, azimuth : azimuth + slab, :] = held_ref[0, m]
        column_ref[m, azimuth + slab : azimuth + PAD, :] = held_ref[1, m, : PAD - slab]

    def remap(g, total):
        start = lax.rem(g * slab - shift - 3 + 2 * azimuth, azimuth)
        for r in range(0, slab, 8):
            both = []
            for m in range(members):
                value = weights[0] * column_ref[m, pl.ds(start + r, 8), :]
                for k in range(1, 6):
                    value += weights[k] * column_ref[m, pl.ds(start + r + k, 8), :]
                moved_ref[g, m, r : r + 8, :] = value
                both.append(value)
            total += both[0] * both[1]
        return total

    total = lax.fori_loop(0, slabs, remap, jnp.zeros((8, vertical), jnp.float32), unroll=2)
    product = jnp.sum(total, axis=0, keepdims=True)
    sums_ref[0:1, :] = jnp.where(team == 0, product, 0.0)
    sums_ref[1:2, :] = jnp.where(team == 1, -product, 0.0)


def remap(place, shifts, fraction, held):
    slabs, members, slab, vertical = held.shape
    smem = pl.BlockSpec(memory_space=pltpu.SMEM)
    vmem = pl.BlockSpec(memory_space=pltpu.VMEM)
    return pl.pallas_call(
        remap_kernel,
        in_specs=[smem, smem, smem, vmem],
        out_specs=[vmem, vmem],
        out_shape=[
            jax.ShapeDtypeStruct(held.shape, held.dtype),
            jax.ShapeDtypeStruct((2, vertical), jnp.float32),
        ],
        scratch_shapes=[pltpu.VMEM((members, slabs * slab + PAD, vertical), jnp.float32)],
        compiler_params=pltpu.CompilerParams(vmem_limit_bytes=SCOPE),
        name="remap",
    )(place, shifts, fraction, held)


def on_device(fields, shifts, fraction):
    components, columns, slab, vertical = fields.shape
    slabs = lax.axis_size(GY)
    place = lax.axis_index(GY).astype(jnp.int32).reshape(1)
    packed = pack(fields).reshape(components * columns, slab, vertical)
    held = lax.all_to_all(packed, GY, split_axis=0, concat_axis=0, tiled=True)
    moved, sums = remap(place, shifts, fraction, held.reshape(slabs, 2, slab, vertical))
    returned = lax.all_to_all(
        moved.reshape(components * columns, slab, vertical), GY, split_axis=0, concat_axis=0, tiled=True
    )
    remapped = unpack(returned.reshape(4, columns, 2, slab, vertical))
    for axis in GY + GX:
        sums = lax.psum(sums, axis)
    cells = columns * lax.axis_size(GX) * slab * slabs
    return remapped, sums / math.sqrt(cells)


def solution(mesh):
    split = Mesh(mesh.devices.reshape(8, 2, 4, 2, 2), GY + GX)
    placed = (P(None, GX, GY, None), P(GX), P(GX))
    return jax.shard_map(
        on_device,
        mesh=split,
        in_specs=placed,
        out_specs=(P(None, GX, GY, None), P()),
        check_vma=False,
    )
```

time: 244 us -> 163 us (0.67)
  local copies, waits for them, and re-layouts: 53.1 us -> 4.22 us
  other arithmetic: 30.1 us -> 0.57 us
  blocking collectives: 97.3 us -> 82 us
  starting transfers between devices: 13.9 us -> 21.1 us
  Pallas kernels: 0 us -> 5.43 us
    all_to_all x1 -> x0, blocking collectives: 54.5 us -> none  [on_device(): lax.all_to_all(moved, GY, split_axis=1, concat_axis=0, tiled=True)]
    gather x8 -> x0, local copies, waits for them, and re-layouts: 42 us -> none
    psum x5, blocking collectives: 42.8 us -> 82 us  [on_device(): sums = lax.psum(sums, axis)]
    concatenate x1 -> x0, other arithmetic: 20.4 us -> none  [on_device(): doubled = jnp.concatenate([flat, flat, flat[:, :4 * vertical]], axis=1)]
    all_to_all x1 -> x2, starting transfers between devices: 13.9 us -> 21.1 us  [the longest x1 13.6 us: on_device(): held = lax.all_to_all(packed, GY, split_axis=0, concat_axis=0, tiled=True)]
    pallas_call x0 -> x3, Pallas kernels: none -> 5.43 us  [the longest x1 3.08 us: unpack(): pl.pallas_call(copy_block, grid=(4, 2), in_specs=[pl.BlockSpec((1, column...]
    unnamed x7 -> x10, local copies, waits for them, and re-layouts: 7.7 us -> 4.22 us
    all_to_all x3 -> x0, local copies, waits for them, and re-layouts: 3.39 us -> none  [the longest x1 1.76 us: on_device(): lax.all_to_all(stacked, GY, split_axis=0, concat_axis=1, tiled=True)]
  transfers between devices with their start and end apart: 1 -> 2, of which waited for: 1 -> 1; matrix products, arithmetic and copies ran while one was open for 0% -> 0% of each run, Pallas kernels for 0% -> 0%
where the time goes in v1:
time: 163 us
  blocking collectives  82 us (50%)
  waiting for transfers between devices  48.6 us (30%)
  starting transfers between devices  21.1 us (13%)
  Pallas kernels  5.43 us (3%)
  local copies, waits for them, and re-layouts  4.22 us (3%)
    psum x5, blocking collectives, on_device(): sums = lax.psum(sums, axis)  82 us
    all_to_all x1, waiting for transfers between devices, on_device(): held = lax.all_to_all(packed, GY, split_axis=0, concat_axis=0, tiled=True)  48.6 us
    all_to_all x1, starting transfers between devices, on_device(): held = lax.all_to_all(packed, GY, split_axis=0, concat_axis=0, tiled=True)  13.6 us
    all_to_all x1, starting transfers between devices, on_device(): lax.all_to_all(moved.reshape(components * columns, slab, vertical), GY, s...  7.5 us
    unnamed x10, local copies, waits for them, and re-layouts  4.22 us
  transfers between devices with their start and end apart: 2, of which 1 were waited for; matrix products, arithmetic and copies ran while one was open for 0% of the time, Pallas kernels for 0%

profile of v1, /device:TPU:1, one launch (start us, length us, event | category | flops | bytes accessed | tf_op | source)
XLA Modules:
  0.0 162.6 jit_solution(8444024463572890376)
XLA Ops:
  0.6 0.0 copy-start.1
  0.6 1.6 copy-done.1
  2.2 0.4 pack.1
  2.7 0.0 copy-start
  2.7 1.3 copy-done
  4.0 0.0 copy-start.3
  4.0 0.0 copy-start.4
  4.0 13.6 %all-to-all-start = ((f32[128,32,128]{2,1,0:T(8,128)}), f32[128,32,128]{2,1,0:T(8,128)S(1)}, u32[]{:S(2)}, u32[]{:S(2)}) async-start(f32[128,32,128]{2,1,0:T(8,128)} %bitcast.6), calls=%async_computation | async-start | bytes 4194304 | tf_op jit(solution)/shard_map/all_to_all | solution.py:131
  17.6 48.6 %all-to-all-done = f32[128,32,128]{2,1,0:T(8,128)S(1)} async-done(((f32[128,32,128]{2,1,0:T(8,128)}), f32[128,32,128]{2,1,0:T(8,128)S(1)}, u32[]{:S(2)}, u32[]{:S(2)}) %all-to-all-start) | async-done | bytes 2097184 | tf_op jit(solution)/shard_map/all_to_all | solution.py:131
  66.2 0.0 copy-done.3
  66.3 0.0 copy-done.4
  66.3 1.9 %remap.1 = (f32[64,2,32,128]{3,2,1,0:T(8,128)S(1)}, f32[2,128]{1,0:T(2,128)S(1)}) custom-call(s32[1]{0:T(128)} %bitcast.place_ref, s32[16]{0:T(128)S(1)} %copy-done.3, f32[16]{0:T(128)S(1)} %copy-done.4, f32[64,2,32,128]{3,2,1,0:T(8,128)S(1)} %bitcast.5), custom_call_target="tpu_custom_call" | custom-call | tf_op jit(solution)/shard_map/remap/pallas_call | solution.py:112
  68.2 0.0 copy-start.2
  68.2 1.3 copy-done.2
  69.5 7.5 %all-to-all-start.1 = ((f32[128,32,128]{2,1,0:T(8,128)}), f32[128,32,128]{2,1,0:T(8,128)S(1)}, u32[]{:S(2)}, u32[]{:S(2)}) async-start(f32[128,32,128]{2,1,0:T(8,128)} %bitcast.8), calls=%async_computation.1 | async-start | bytes 4194304 | tf_op jit(solution)/shard_map/all_to_all | solution.py:133
  77.0 52.7 %psum.35 = f32[2,128]{1,0:T(2,128)S(1)} all-reduce(f32[2,128]{1,0:T(2,128)S(1)} %get-tuple-element.5), channel_id=1, replica_groups=mesh['gy_0'=8,'gy_1'=2,'gy_2'=4,'gx_0'=2,'gx_1'=2] {'gy_0'}, use_global_device_ids=true, to_apply=%region_0.0 | all-reduce | flops 256 | bytes 2048 | tf_op jit(solution)/shard_map/psum | solution.py:138
  129.7 3.8 %psum.36 = f32[2,128]{1,0:T(2,128)S(1)} all-reduce(f32[2,128]{1,0:T(2,128)S(1)} %psum.35), channel_id=1, replica_groups=mesh['gy_0'=8,'gy_1'=2,'gy_2'=4,'gx_0'=2,'gx_1'=2] {'gy_1'}, use_global_device_ids=true, to_apply=%region_1.0 | all-reduce | flops 256 | bytes 2048 | tf_op jit(solution)/shard_map/psum | solution.py:138
  133.5 8.7 %psum.37 = f32[2,128]{1,0:T(2,128)S(1)} all-reduce(f32[2,128]{1,0:T(2,128)S(1)} %psum.36), channel_id=1, replica_groups=mesh['gy_0'=8,'gy_1'=2,'gy_2'=4,'gx_0'=2,'gx_1'=2] {'gy_2'}, use_global_device_ids=true, to_apply=%region_2.0 | all-reduce | flops 256 | bytes 2048 | tf_op jit(solution)/shard_map/psum | solution.py:138
  142.1 5.3 %psum.38 = f32[2,128]{1,0:T(2,128)S(1)} all-reduce(f32[2,128]{1,0:T(2,128)S(1)} %psum.37), channel_id=1, replica_groups=mesh['gy_0'=8,'gy_1'=2,'gy_2'=4,'gx_0'=2,'gx_1'=2] {'gx_0'}, use_global_device_ids=true, to_apply=%region_3.0 | all-reduce | flops 256 | bytes 2048 | tf_op jit(solution)/shard_map/psum | solution.py:138
  147.4 11.6 %psum.39 = f32[2,128]{1,0:T(2,128)S(1)} all-reduce(f32[2,128]{1,0:T(2,128)S(1)} %psum.38), channel_id=1, replica_groups=mesh['gy_0'=8,'gy_1'=2,'gy_2'=4,'gx_0'=2,'gx_1'=2] {'gx_1'}, use_global_device_ids=true, to_apply=%region_4.0 | all-reduce | flops 256 | bytes 2048 | tf_op jit(solution)/shard_map/psum | solution.py:138
  159.0 0.6 broadcast_multiply_fusion
  159.5 0.0 all-to-all-done.1
  159.5 3.1 %unpack.1 = f32[8,16,32,128]{3,2,1,0:T(8,128)} custom-call(f32[4,16,2,32,128]{4,3,2,1,0:T(8,128)S(1)} %bitcast.7), custom_call_target="tpu_custom_call" | custom-call | tf_op jit(solution)/shard_map/unpack/pallas_call | solution.py:59
Async XLA Ops:
  0.6 1.6 copy-start.1
  2.7 1.3 copy-start
  4.0 62.3 %copy-start.3 = (s32[16]{0:T(128)S(1)}, s32[16]{0:T(128)}, u32[]{:S(2)}) copy-start(s32[16]{0:T(128)} %shifts_ref.1) | copy-start | bytes 196
  4.0 62.3 %copy-start.4 = (f32[16]{0:T(128)S(1)}, f32[16]{0:T(128)}, u32[]{:S(2)}) copy-start(f32[16]{0:T(128)} %fraction_ref.1) | copy-start | bytes 196
  4.0 62.3 %all-to-all-start = ((f32[128,32,128]{2,1,0:T(8,128)}), f32[128,32,128]{2,1,0:T(8,128)S(1)}, u32[]{:S(2)}, u32[]{:S(2)}) async-start(f32[128,32,128]{2,1,0:T(8,128)} %bitcast.6), calls=%async_computation | async-start | bytes 4194304 | tf_op jit(solution)/shard_map/all_to_all | solution.py:131
  68.2 1.3 copy-start.2
  69.5 90.0 %all-to-all-start.1 = ((f32[128,32,128]{2,1,0:T(8,128)}), f32[128,32,128]{2,1,0:T(8,128)S(1)}, u32[]{:S(2)}, u32[]{:S(2)}) async-start(f32[128,32,128]{2,1,0:T(8,128)} %bitcast.8), calls=%async_computation.1 | async-start | bytes 4194304 | tf_op jit(solution)/shard_map/all_to_all | solution.py:133
